TPU v7x, 32 devices: a whole 2x2x4 slice. The times are simulated.
32 devices in a mesh: par: 4 (over x, core), freq: 8 (over z, y).
Axes of the slice: x: 2, y: 2, z: 4, core: 2. Of those that a mesh axis runs over, the one named last changes fastest.
Arguments:
- probes: bfloat16 [64, 600, 420], P('freq'), may hold values from -6 to 6
- map_real: bfloat16 [112, 600, 1024], P('freq', None, 'par'), may hold values from -0.1875 to 0.1875
- map_imag: bfloat16 [112, 600, 1024], P('freq', None, 'par'), may hold values from -0.1875 to 0.1875
- prior_var: float32 [1024], P('par'), may hold values from 0.05 to 13, as said below
Outputs:
- applied: bfloat16 [64, 600, 420], P('freq')
Inputs may be any that keep to these rules, and one draw needn't show every extreme that they name: `prior_var`: prior variances are positive.
All inputs are finite; a program needn't handle non-finite values.
Results may differ from a plain program's by a relative error of at most 0.014.
Values may be sent and summed in bfloat16 or wider, within the bound.
A program may use at most 64 MiB of HBM per device.

v0:
```python
import jax
import jax.numpy as jnp
from jax import lax
from jax.sharding import PartitionSpec as P

SENSORS = 600
STEPS = 420
PERIOD = 840
PROBES = 64
noise_ratio = 0.5


def split_product(left, table):
    upper = table.astype(jnp.bfloat16)
    lower = (table - upper.astype(jnp.float32)).astype(jnp.bfloat16)
    return jnp.dot(left, upper, preferred_element_type=jnp.float32) + jnp.dot(
        left, lower, preferred_element_type=jnp.float32
    )


def shards(probes, map_real, map_imag, prior_var):
    freq_count = lax.axis_size("freq")
    bins_dev = map_real.shape[0]
    probe_block = probes.shape[0]
    total_bins = bins_dev * freq_count
    time_steps = jnp.arange(STEPS, dtype=jnp.int32)
    bin_index = jnp.arange(total_bins, dtype=jnp.int32)
    product_index = time_steps[:, None] * bin_index[None, :] % PERIOD
    angles = product_index.astype(jnp.float32) * (2.0 * jnp.pi / PERIOD)
    norm_scale = 1.0 / jnp.sqrt(jnp.float32(PERIOD))
    cosines = jnp.cos(angles) * norm_scale
    sines = jnp.sin(angles) * norm_scale
    forward = jnp.stack([cosines, -sines], axis=2).reshape(STEPS, 2 * total_bins)
    all_weight = jnp.where(bin_index == 0, 1.0, 2.0).astype(jnp.float32)
    inverse = jnp.stack([cosines * all_weight[None, :], -sines * all_weight[None, :]], axis=2)
    inverse = inverse.reshape(STEPS, 2 * total_bins).T
    flattened = probes.reshape(probe_block * SENSORS, STEPS)
    spectrum = split_product(flattened, forward).astype(jnp.bfloat16)
    spectrum = spectrum.reshape(probe_block, SENSORS, 2 * total_bins)
    exchanged = lax.all_to_all(spectrum, "freq", split_axis=2, concat_axis=0, tiled=True)
    all_probes = exchanged.shape[0]
    operand = exchanged.reshape(all_probes, SENSORS, bins_dev, 2).transpose(2, 1, 3, 0)
    operand = operand.reshape(bins_dev, SENSORS, 2 * all_probes)
    left_real = jnp.einsum("ksp,ksc->kpc", map_real, operand, preferred_element_type=jnp.float32)
    left_imag = jnp.einsum("ksp,ksc->kpc", map_imag, operand, preferred_element_type=jnp.float32)
    u_real = left_real[..., :all_probes] + left_imag[..., all_probes:]
    u_imag = left_real[..., all_probes:] - left_imag[..., :all_probes]
    global_bin = lax.axis_index("freq") * bins_dev + jnp.arange(bins_dev, dtype=jnp.int32)
    bin_weight = jnp.where(global_bin == 0, 1.0, 2.0).astype(jnp.float32)
    quadratic = jnp.sum(
        bin_weight[:, None, None] * prior_var[None, :, None] * (u_real * u_real + u_imag * u_imag)
    )
    trace_est = lax.psum(quadratic, ("par", "freq")) / (PROBES * SENSORS * STEPS)
    scaled = (jnp.concatenate([u_real, u_imag], axis=-1) * prior_var[None, :, None]).astype(
        jnp.bfloat16
    )
    right_real = jnp.einsum("ksp,kpc->ksc", map_real, scaled, preferred_element_type=jnp.float32)
    right_imag = jnp.einsum("ksp,kpc->ksc", map_imag, scaled, preferred_element_type=jnp.float32)
    w_partial = jnp.concatenate(
        [
            right_real[..., :all_probes] - right_imag[..., all_probes:],
            right_real[..., all_probes:] + right_imag[..., :all_probes],
        ],
        axis=-1,
    )
    summed = lax.psum(w_partial.astype(jnp.bfloat16), "par")
    outgoing = summed.reshape(bins_dev, SENSORS, 2, all_probes).transpose(3, 1, 0, 2)
    outgoing = outgoing.reshape(all_probes, SENSORS, 2 * bins_dev)
    by_probe = lax.all_to_all(outgoing, "freq", split_axis=0, concat_axis=2, tiled=True)
    by_rows = by_probe.reshape(probe_block * SENSORS, 2 * total_bins)
    response = split_product(by_rows, inverse).reshape(probe_block, SENSORS, STEPS)
    return (response + noise_ratio * trace_est * probes.astype(jnp.float32)).astype(jnp.bfloat16)


def solution(mesh):
    placed = (P("freq", None, None), P("freq", None, "par"), P("freq", None, "par"), P("par"))
    return jax.shard_map(
        shards, mesh=mesh, in_specs=placed, out_specs=P("freq", None, None), check_vma=False
    )
```

profile of v0, /device:TPU:0, one launch (start us, length us, event | category | flops | bytes accessed | tf_op | source)
XLA Modules:
  0.0 288.2 jit_solution(12911080688204210552)
XLA Ops:
  6.5 7.8 %multiply_negate_fusion = (f32[420,112,1]{0,2,1:T(1,128)S(1)}, f32[420,112,1]{0,2,1:T(1,128)S(1)}) fusion(), kind=kLoop, calls=%fused_computation.29 | loop fusion | flops 564480 | bytes 376320 | tf_op jit(solution)/shard_map/neg | solution.py:33
  14.4 0.5 subtract_convert_fusion
  14.8 0.4 fusion.9
  15.7 8.0 %reshape.201 = bf16[4800,420]{0,1:T(8,128)(2,1)} reshape(bf16[8,600,420]{1,0,2:T(8,128)(2,1)} %param.4) | data formatting | bytes 8064000 | tf_op jit(solution)/shard_map/reshape | solution.py:37
  23.6 3.6 %fusion.20 = f32[224,4800]{1,0:T(8,128)S(1)} fusion(bf16[420,224]{0,1:T(8,128)(2,1)S(1)} %convert_element_type.96, bf16[4800,420]{0,1:T(8,128)(2,1)} %reshape.201), kind=kOutput, calls=%fused_computation.44 | convolution fusion | flops 903168000 | bytes 8520960 | tf_op jit(solution)/shard_map/dot_general | solution.py:16
  27.3 1.3 fusion.1
  28.6 3.8 %reshape.202 = bf16[8,600,224]{1,0,2:T(8,128)(2,1)} reshape(bf16[4800,224]{0,1:T(8,128)(2,1)S(1)} %fusion.1) | data formatting | bytes 4300800 | tf_op jit(solution)/shard_map/reshape | solution.py:39
  32.4 7.4 %all-to-all-start = ((bf16[8,600,224]{1,0,2:T(8,128)(2,1)}), bf16[8,600,224]{1,0,2:T(8,128)(2,1)S(1)}, u32[]{:S(2)}, u32[]{:S(2)}) async-start(bf16[8,600,224]{1,0,2:T(8,128)(2,1)} %reshape.202), calls=%async_computation | async-start | bytes 4587520 | tf_op jit(solution)/shard_map/all_to_all | solution.py:40
  39.9 0.2 all-reduce.2.cloned.1.call-start
  40.2 52.1 %all-to-all-done = bf16[8,600,224]{1,0,2:T(8,128)(2,1)S(1)} async-done(((bf16[8,600,224]{1,0,2:T(8,128)(2,1)}), bf16[8,600,224]{1,0,2:T(8,128)(2,1)S(1)}, u32[]{:S(2)}, u32[]{:S(2)}) %all-to-all-start) | async-done | bytes 2150432 | tf_op jit(solution)/shard_map/all_to_all | solution.py:40
  92.3 0.3 copy.20
  92.7 3.3 %convolution_bitcast_fusion.2 = f32[14,256,128]{1,2,0:T(8,128)S(1)} fusion(bf16[14,600,128]{1,2,0:T(8,128)(2,1)S(1)} %bitcast.74, bf16[14,600,256]{2,1,0:T(8,128)(2,1)} %param.6), kind=kOutput, calls=%fused_computation.15 | convolution fusion | flops 550502400 | bytes 8286208 | tf_op jit(solution)/shard_map/ksp,ksc->kpc/dot_general | solution.py:45
  96.0 0.9 convolution_bitcast_fusion.3
  97.0 1.1 multiply_reduce_fusion
  98.1 1.3 convolution_bitcast_fusion
  99.4 1.3 convolution_bitcast_fusion.1
  100.7 2.4 fusion.3
  103.2 1.2 pad_maximum_fusion
  104.4 3.4 %copy.25 = bf16[14,600,128]{1,2,0:T(8,128)(2,1)} copy(bf16[14,600,128]{2,1,0:T(8,128)(2,1)S(1)} %pad_maximum_fusion) | data formatting | bytes 4300800 | tf_op jit(solution)/shard_map/concatenate | solution.py:59
  107.8 53.8 %all-reduce.2.cloned.1.call-done = bf16[64,600,28]{1,0,2:T(8,128)(2,1)} async-done(((bf16[64,600,28]{1,0,2:T(8,128)(2,1)}), bf16[64,600,28]{1,0,2:T(8,128)(2,1)}) %all-reduce.2.cloned.1.call-update) | async-done | bytes 2150416 | tf_op jit(solution)/shard_map/psum | solution.py:66
  161.6 4.5 %copy.26 = bf16[64,600,28]{1,2,0:T(8,128)(2,1)} copy(bf16[64,600,28]{1,0,2:T(8,128)(2,1)} %all-reduce.2.cloned.1.call-done) | data formatting | bytes 4300800 | tf_op jit(solution)/shard_map/psum | solution.py:66
  166.0 5.5 %all-to-all-start.1 = ((bf16[64,600,28]{1,2,0:T(8,128)(2,1)}), bf16[64,600,28]{1,2,0:T(8,128)(2,1)S(1)}, u32[]{:S(2)}, u32[]{:S(2)}) async-start(bf16[64,600,28]{1,2,0:T(8,128)(2,1)} %copy.26), calls=%async_computation.1 | async-start | bytes 5242880 | tf_op jit(solution)/shard_map/all_to_all | solution.py:69
  171.6 8.0 %broadcast_multiply_fusion = (f32[420,112,1]{0,2,1:T(1,128)S(1)}, f32[420,112,1]{0,2,1:T(1,128)S(1)}) fusion(f32[112]{0:T(128)S(1)} %compare_select_fusion.1, f32[112]{0:T(128)S(1)} %broadcast_multiply_fusion.4), kind=kLoop, calls=%fused_computation.31 | loop fusion | flops 611520 | bytes 377216 | tf_op jit(solution)/shard_map/mul | solution.py:35
  179.6 0.4 pad_maximum_fusion.2
  180.1 0.3 reshape.208
  180.4 70.5 %psum.15 = f32[]{:T(128)} all-reduce(f32[]{:T(128)} %get-tuple-element.5), channel_id=1, replica_groups=mesh['par'=4,'freq'=8] {'par','freq'}, use_global_device_ids=true, to_apply=%region_2.3 | all-reduce | flops 1 | bytes 8 | tf_op jit(solution)/shard_map/psum | solution.py:53
  251.5 2.2 copy.33
  253.8 3.6 %reshape.207 = bf16[4800,224]{0,1:T(8,128)(2,1)S(1)} reshape(bf16[8,600,8,28]{1,0,3,2:T(8,128)(2,1)} %bitcast.83) | data formatting | bytes 4300800 | tf_op jit(solution)/shard_map/reshape | solution.py:70
  257.4 1.3 fusion.17
  258.6 4.6 %convolution_add_fusion = f32[4800,420]{0,1:T(8,128)} fusion(f32[4800,420]{0,1:T(8,128)S(1)} %fusion.17, bf16[4800,224]{0,1:T(8,128)(2,1)S(1)} %reshape.207, f32[420,224]{0,1:T(8,128)S(1)} %reshape.208), kind=kOutput, calls=%fused_computation.1 | convolution fusion | flops 905560320 | bytes 18654720 | tf_op jit(solution)/shard_map/dot_general | solution.py:16
  263.2 10.4 %reshape.209 = f32[8,600,420]{1,0,2:T(8,128)} reshape(f32[4800,420]{0,1:T(8,128)} %convolution_add_fusion) | data formatting | bytes 16128000 | tf_op jit(solution)/shard_map/reshape | solution.py:71
  273.6 7.7 %add_convert_fusion = bf16[8,600,420]{1,0,2:T(8,128)(2,1)} fusion(f32[8,600,420]{1,0,2:T(8,128)} %reshape.209, bf16[8,600,420]{1,0,2:T(8,128)(2,1)} %param.4, f32[]{:T(128)S(6)} %mul_shard_map.3), kind=kLoop, calls=%fused_computation | loop fusion | flops 8064000 | bytes 16128004 | tf_op jit(solution)/shard_map/convert_element_type | solution.py:72
  (22 shorter events, 0.5 us)
Async XLA Ops:
  23.6 3.6 %copy-start = (bf16[4800,420]{0,1:T(8,128)(2,1)S(1)}, bf16[4800,420]{0,1:T(8,128)(2,1)}, u32[]{:S(2)}) copy-start(bf16[4800,420]{0,1:T(8,128)(2,1)} %reshape.201) | copy-start | bytes 12096004
  28.6 11.5 %copy-start.1 = (f32[256]{0:T(256)S(1)}, f32[256]{0:T(256)}, u32[]{:S(2)}) copy-start(f32[256]{0:T(256)} %param.7) | copy-start | bytes 3076
  32.4 63.6 %slice-start.2 = ((s8[4300800]{0:T(1024)(128)(4,1)}), s8[106496]{0:T(1024)(128)(4,1)S(1)}, s32[]{:S(2)}) async-start(s8[4300800]{0:T(1024)(128)(4,1)} %bitcast.78), calls=%async_computation.5 | async-start | bytes 212992
  32.4 59.9 %all-to-all-start = ((bf16[8,600,224]{1,0,2:T(8,128)(2,1)}), bf16[8,600,224]{1,0,2:T(8,128)(2,1)S(1)}, u32[]{:S(2)}, u32[]{:S(2)}) async-start(bf16[8,600,224]{1,0,2:T(8,128)(2,1)} %reshape.202), calls=%async_computation | async-start | bytes 4587520 | tf_op jit(solution)/shard_map/all_to_all | solution.py:40
  39.9 121.7 %all-reduce.2.cloned.1.call-start = ((), (), s32[]{:S(2)}) async-start(), calls=%async_computation.2 | async-start | bytes 4587520 | tf_op jit(solution)/shard_map/psum | solution.py:66
  92.3 3.7 %slice-start.3 = ((s8[4300800]{0:T(1024)(128)(4,1)}), s8[4194304]{0:T(1024)(128)(4,1)S(1)}, s32[]{:S(2)}) async-start(s8[4300800]{0:T(1024)(128)(4,1)} %bitcast.78), calls=%async_computation.6 | async-start | bytes 8388608
  92.7 5.4 %slice-start = ((s8[4300800]{0:T(1024)(128)(4,1)}), s8[4194304]{0:T(1024)(128)(4,1)S(1)}, s32[]{:S(2)}) async-start(s8[4300800]{0:T(1024)(128)(4,1)} %bitcast.76), calls=%async_computation.3 | async-start | bytes 8388608
  96.0 2.0 slice-start.1
  166.0 85.5 %all-to-all-start.1 = ((bf16[64,600,28]{1,2,0:T(8,128)(2,1)}), bf16[64,600,28]{1,2,0:T(8,128)(2,1)S(1)}, u32[]{:S(2)}, u32[]{:S(2)}) async-start(bf16[64,600,28]{1,2,0:T(8,128)(2,1)} %copy.26), calls=%async_computation.1 | async-start | bytes 5242880 | tf_op jit(solution)/shard_map/all_to_all | solution.py:69
Sparse Core Ops, SparseCore 0:
  107.9 53.6 all-reduce.1
where the time goes:
time: 289 us; the launch traced here: 288 us
  waiting for transfers between devices  106 us (37%)
  blocking collectives  70.5 us (24%)
  local copies, waits for them, and re-layouts  36.9 us (13%)
  other arithmetic  29.7 us (10%)
  matrix products  17.7 us (6%)
  between operations  14.3 us (5%)
  starting transfers between devices  13.2 us (5%)
    psum x1, blocking collectives, shards(): lax.psum(quadratic, ('par', 'freq')) / (PROBES * SENSORS * STEPS)  70.5 us
    psum x1, waiting for transfers between devices, shards(): summed = lax.psum(w_partial.astype(jnp.bfloat16), 'par')  53.8 us
    all_to_all x1, waiting for transfers between devices, shards(): lax.all_to_all(spectrum, 'freq', split_axis=2, concat_axis=0, tiled=True)  52.1 us
    reshape x1, local copies, waits for them, and re-layouts, shards(): split_product(by_rows, inverse).reshape(probe_block, SENSORS, STEPS)  10.4 us
    mul x1, other arithmetic, shards(): -sines * all_weight[None, :]  8.04 us
    reshape x1, local copies, waits for them, and re-layouts, shards(): flattened = probes.reshape(probe_block * SENSORS, STEPS)  7.96 us
    neg x1, other arithmetic, shards(): -sines  7.81 us
    convert_element_type x1, other arithmetic, shards(): (response + noise_ratio * trace_est * probes.astype(jnp.float32)).astype(...  7.71 us
  transfers between devices with their start and end apart: 3, of which 2 were waited for; matrix products, arithmetic and copies ran while one was open for 3% of the time, Pallas kernels for 0%

commit v1 on v0

--- a/solution.py
+++ b/solution.py
@@ -1,3 +1,4 @@
+import functools
 import jax
 import jax.numpy as jnp
 from jax import lax
@@ -8,6 +9,15 @@
 PERIOD = 840
 PROBES = 64
 noise_ratio = 0.5
+
+
+def _resolve_turns(local_x, shard_axis):
+    mixed_arr = lax.all_gather(local_x, shard_axis)
+    now = jnp.sum(mixed_arr, 0)
+    return now
+
+
+ports_move = functools.partial(_resolve_turns, shard_axis="par")
 
 
 def split_product(left, table):
@@ -63,7 +73,7 @@
         ],
         axis=-1,
     )
-    summed = lax.psum(w_partial.astype(jnp.bfloat16), "par")
+    summed = ports_move(w_partial.astype(jnp.bfloat16))
     outgoing = summed.reshape(bins_dev, SENSORS, 2, all_probes).transpose(3, 1, 0, 2)
     outgoing = outgoing.reshape(all_probes, SENSORS, 2 * bins_dev)
     by_probe = lax.all_to_all(outgoing, "freq", split_axis=0, concat_axis=2, tiled=True)

time: 289 us -> 301 us (1.042)
  other arithmetic: 29.7 us -> 37.7 us
  waiting for transfers between devices: 106 us -> 111 us
    all_gather x0 -> x1, waiting for transfers between devices: none -> 58.7 us  [_resolve_turns(): mixed_arr = lax.all_gather(local_x, shard_axis)]
    psum x1 -> x0, waiting for transfers between devices: 53.8 us -> none  [shards(): summed = lax.psum(w_partial.astype(jnp.bfloat16), 'par')]
    reduce_sum x0 -> x1, other arithmetic: none -> 6.65 us  [_resolve_turns(): now = jnp.sum(mixed_arr, 0)]
    psum x1 -> x0, local copies, waits for them, and re-layouts: 4.46 us -> none  [shards(): summed = lax.psum(w_partial.astype(jnp.bfloat16), 'par')]
    concatenate x1 -> x2, other arithmetic: 1.18 us -> 4.96 us  [shards(): jnp.concatenate([right_real[..., :all_probes] - right_imag[..., all_probe...]
    concatenate x1 -> x0, local copies, waits for them, and re-layouts: 3.37 us -> none  [shards(): jnp.concatenate([right_real[..., :all_probes] - right_imag[..., all_probe...]
    reduce_sum x0 -> x1, local copies, waits for them, and re-layouts: none -> 3.27 us  [_resolve_turns(): now = jnp.sum(mixed_arr, 0)]
where the time goes in v1:
time: 301 us; the launch traced here: 300 us
  waiting for transfers between devices  111 us (37%)
  blocking collectives  71.2 us (24%)
  other arithmetic  37.7 us (13%)
  local copies, waits for them, and re-layouts  35.1 us (12%)
  matrix products  17.7 us (6%)
  between operations  14.3 us (5%)
  starting transfers between devices  13.2 us (4%)
    psum x1, blocking collectives, shards(): lax.psum(quadratic, ('par', 'freq')) / (PROBES * SENSORS * STEPS)  71.2 us
    all_gather x1, waiting for transfers between devices, _resolve_turns(): mixed_arr = lax.all_gather(local_x, shard_axis)  58.7 us
    all_to_all x1, waiting for transfers between devices, shards(): lax.all_to_all(spectrum, 'freq', split_axis=2, concat_axis=0, tiled=True)  52.1 us
    reshape x1, local copies, waits for them, and re-layouts, shards(): split_product(by_rows, inverse).reshape(probe_block, SENSORS, STEPS)  10.4 us
    mul x1, other arithmetic, shards(): -sines * all_weight[None, :]  8.04 us
    reshape x1, local copies, waits for them, and re-layouts, shards(): flattened = probes.reshape(probe_block * SENSORS, STEPS)  7.96 us
    neg x1, other arithmetic, shards(): -sines  7.81 us
    convert_element_type x1, other arithmetic, shards(): (response + noise_ratio * trace_est * probes.astype(jnp.float32)).astype(...  7.71 us
  transfers between devices with their start and end apart: 3, of which 2 were waited for; matrix products, arithmetic and copies ran while one was open for 3% of the time, Pallas kernels for 0%

profile of v1, /device:TPU:0, one launch (start us, length us, event | category | flops | bytes accessed | tf_op | source)
XLA Modules:
  0.0 300.0 jit_solution(15637428624718160441)
XLA Ops:
  6.5 7.8 %multiply_negate_fusion = (f32[420,112,1]{0,2,1:T(1,128)S(1)}, f32[420,112,1]{0,2,1:T(1,128)S(1)}) fusion(), kind=kLoop, calls=%fused_computation.31 | loop fusion | flops 564480 | bytes 376320 | tf_op jit(solution)/shard_map/neg | solution.py:43
  14.4 0.5 subtract_convert_fusion
  14.8 0.4 fusion.11
  15.7 8.0 %reshape.232 = bf16[4800,420]{0,1:T(8,128)(2,1)} reshape(bf16[8,600,420]{1,0,2:T(8,128)(2,1)} %param.4) | data formatting | bytes 8064000 | tf_op jit(solution)/shard_map/reshape | solution.py:47
  23.6 3.6 %fusion.22 = f32[224,4800]{1,0:T(8,128)S(1)} fusion(bf16[420,224]{0,1:T(8,128)(2,1)S(1)} %convert_element_type.105, bf16[4800,420]{0,1:T(8,128)(2,1)} %reshape.232), kind=kOutput, calls=%fused_computation.46 | convolution fusion | flops 903168000 | bytes 8520960 | tf_op jit(solution)/shard_map/dot_general | solution.py:26
  27.3 1.3 fusion.1
  28.6 3.8 %reshape.233 = bf16[8,600,224]{1,0,2:T(8,128)(2,1)} reshape(bf16[4800,224]{0,1:T(8,128)(2,1)S(1)} %fusion.1) | data formatting | bytes 4300800 | tf_op jit(solution)/shard_map/reshape | solution.py:49
  32.4 7.4 %all-to-all-start = ((bf16[8,600,224]{1,0,2:T(8,128)(2,1)}), bf16[8,600,224]{1,0,2:T(8,128)(2,1)S(1)}, u32[]{:S(2)}, u32[]{:S(2)}) async-start(bf16[8,600,224]{1,0,2:T(8,128)(2,1)} %reshape.233), calls=%async_computation | async-start | bytes 4587520 | tf_op jit(solution)/shard_map/all_to_all | solution.py:50
  40.2 52.1 %all-to-all-done = bf16[8,600,224]{1,0,2:T(8,128)(2,1)S(1)} async-done(((bf16[8,600,224]{1,0,2:T(8,128)(2,1)}), bf16[8,600,224]{1,0,2:T(8,128)(2,1)S(1)}, u32[]{:S(2)}, u32[]{:S(2)}) %all-to-all-start) | async-done | bytes 2150432 | tf_op jit(solution)/shard_map/all_to_all | solution.py:50
  92.3 0.3 copy.18
  92.7 3.3 %convolution_bitcast_fusion.2 = f32[14,256,128]{1,2,0:T(8,128)S(1)} fusion(bf16[14,600,128]{1,2,0:T(8,128)(2,1)S(1)} %bitcast.78, bf16[14,600,256]{2,1,0:T(8,128)(2,1)} %param.6), kind=kOutput, calls=%fused_computation.17 | convolution fusion | flops 550502400 | bytes 8286208 | tf_op jit(solution)/shard_map/ksp,ksc->kpc/dot_general | solution.py:55
  96.0 0.9 convolution_bitcast_fusion.3
  97.0 1.0 multiply_reduce_fusion
  98.0 1.3 convolution_bitcast_fusion
  99.4 1.3 convolution_bitcast_fusion.1
  100.7 2.4 fusion.4
  103.2 2.5 pad_maximum_fusion
  105.7 58.7 %all-gather.2.cloned.1.call-done = bf16[4,14,600,128]{3,2,1,0:T(8,128)(2,1)} async-done(((bf16[1,14,600,128]{3,2,1,0:T(8,128)(2,1)}), bf16[4,14,600,128]{3,2,1,0:T(8,128)(2,1)}) %all-gather.2.cloned.1.call-update) | async-done | bytes 8601616 | tf_op jit(solution)/shard_map/all_gather | solution.py:15
  164.4 6.7 %reduce_sum.21 = bf16[14,600,128]{2,1,0:T(8,128)(2,1)} reduce(bf16[4,14,600,128]{3,2,1,0:T(8,128)(2,1)} %all-gather.2.cloned.1.call-done, bf16[]{:T(256)} %constant.15.clone.1), dimensions={0}, to_apply=%region_0.1 | reduce | flops 3225600 | bytes 10752002 | tf_op jit(solution)/shard_map/reduce_sum | solution.py:16
  171.0 3.3 %copy.23 = bf16[14,600,128]{1,2,0:T(8,128)(2,1)S(1)} copy(bf16[14,600,128]{2,1,0:T(8,128)(2,1)} %reduce_sum.21) | data formatting | bytes 4300800 | tf_op jit(solution)/shard_map/reduce_sum | solution.py:16
  174.3 2.8 copy.24
  177.1 5.5 %all-to-all-start.1 = ((bf16[64,600,28]{1,2,0:T(8,128)(2,1)}), bf16[64,600,28]{1,2,0:T(8,128)(2,1)S(1)}, u32[]{:S(2)}, u32[]{:S(2)}) async-start(bf16[64,600,28]{1,2,0:T(8,128)(2,1)} %copy.24), calls=%async_computation.1 | async-start | bytes 5242880 | tf_op jit(solution)/shard_map/all_to_all | solution.py:79
  182.7 8.0 %broadcast_multiply_fusion = (f32[420,112,1]{0,2,1:T(1,128)S(1)}, f32[420,112,1]{0,2,1:T(1,128)S(1)}) fusion(f32[112]{0:T(128)S(1)} %compare_select_fusion.1, f32[112]{0:T(128)S(1)} %broadcast_multiply_fusion.4), kind=kLoop, calls=%fused_computation.33 | loop fusion | flops 611520 | bytes 377216 | tf_op jit(solution)/shard_map/mul | solution.py:45
  190.7 0.4 pad_maximum_fusion.2
  191.2 0.3 reshape.239
  191.5 71.2 %psum.7 = f32[]{:T(128)} all-reduce(f32[]{:T(128)} %get-tuple-element.5), channel_id=1, replica_groups=mesh['par'=4,'freq'=8] {'par','freq'}, use_global_device_ids=true, to_apply=%region_2.3 | all-reduce | flops 1 | bytes 8 | tf_op jit(solution)/shard_map/psum | solution.py:63
  263.3 2.2 copy.31
  265.5 3.6 %reshape.238 = bf16[4800,224]{0,1:T(8,128)(2,1)S(1)} reshape(bf16[8,600,8,28]{1,0,3,2:T(8,128)(2,1)} %bitcast.87) | data formatting | bytes 4300800 | tf_op jit(solution)/shard_map/reshape | solution.py:80
  269.1 1.3 fusion.19
  270.4 4.6 %convolution_add_fusion = f32[4800,420]{0,1:T(8,128)} fusion(f32[4800,420]{0,1:T(8,128)S(1)} %fusion.19, bf16[4800,224]{0,1:T(8,128)(2,1)S(1)} %reshape.238, f32[420,224]{0,1:T(8,128)S(1)} %reshape.239), kind=kOutput, calls=%fused_computation.1 | convolution fusion | flops 905560320 | bytes 18654720 | tf_op jit(solution)/shard_map/dot_general | solution.py:26
  275.0 10.4 %reshape.240 = f32[8,600,420]{1,0,2:T(8,128)} reshape(f32[4800,420]{0,1:T(8,128)} %convolution_add_fusion) | data formatting | bytes 16128000 | tf_op jit(solution)/shard_map/reshape | solution.py:81
  285.4 7.7 %add_convert_fusion = bf16[8,600,420]{1,0,2:T(8,128)(2,1)} fusion(f32[8,600,420]{1,0,2:T(8,128)} %reshape.240, bf16[8,600,420]{1,0,2:T(8,128)(2,1)} %param.4, f32[]{:T(128)S(6)} %mul_shard_map.3), kind=kLoop, calls=%fused_computation | loop fusion | flops 8064000 | bytes 16128004 | tf_op jit(solution)/shard_map/convert_element_type | solution.py:82
  (23 shorter events, 0.7 us)
Async XLA Ops:
  23.6 3.6 %copy-start = (bf16[4800,420]{0,1:T(8,128)(2,1)S(1)}, bf16[4800,420]{0,1:T(8,128)(2,1)}, u32[]{:S(2)}) copy-start(bf16[4800,420]{0,1:T(8,128)(2,1)} %reshape.232) | copy-start | bytes 12096004
  28.6 11.5 %copy-start.1 = (f32[256]{0:T(256)S(1)}, f32[256]{0:T(256)}, u32[]{:S(2)}) copy-start(f32[256]{0:T(256)} %param.7) | copy-start | bytes 3076
  32.4 63.6 %slice-start.2 = ((s8[4300800]{0:T(1024)(128)(4,1)}), s8[106496]{0:T(1024)(128)(4,1)S(1)}, s32[]{:S(2)}) async-start(s8[4300800]{0:T(1024)(128)(4,1)} %bitcast.82), calls=%async_computation.5 | async-start | bytes 212992
  32.4 59.9 %all-to-all-start = ((bf16[8,600,224]{1,0,2:T(8,128)(2,1)}), bf16[8,600,224]{1,0,2:T(8,128)(2,1)S(1)}, u32[]{:S(2)}, u32[]{:S(2)}) async-start(bf16[8,600,224]{1,0,2:T(8,128)(2,1)} %reshape.233), calls=%async_computation | async-start | bytes 4587520 | tf_op jit(solution)/shard_map/all_to_all | solution.py:50
  39.9 124.5 %all-gather.2.cloned.1.call-start = ((), (), s32[]{:S(2)}) async-start(), calls=%async_computation.2 | async-start | bytes 10752000 | tf_op jit(solution)/shard_map/all_gather | solution.py:15
  92.3 3.7 %slice-start.3 = ((s8[4300800]{0:T(1024)(128)(4,1)}), s8[4194304]{0:T(1024)(128)(4,1)S(1)}, s32[]{:S(2)}) async-start(s8[4300800]{0:T(1024)(128)(4,1)} %bitcast.82), calls=%async_computation.6 | async-start | bytes 8388608
  92.7 5.4 %slice-start = ((s8[4300800]{0:T(1024)(128)(4,1)}), s8[4194304]{0:T(1024)(128)(4,1)S(1)}, s32[]{:S(2)}) async-start(s8[4300800]{0:T(1024)(128)(4,1)} %bitcast.80), calls=%async_computation.3 | async-start | bytes 8388608
  96.0 2.0 slice-start.1
  177.1 86.2 %all-to-all-start.1 = ((bf16[64,600,28]{1,2,0:T(8,128)(2,1)}), bf16[64,600,28]{1,2,0:T(8,128)(2,1)S(1)}, u32[]{:S(2)}, u32[]{:S(2)}) async-start(bf16[64,600,28]{1,2,0:T(8,128)(2,1)} %copy.24), calls=%async_computation.1 | async-start | bytes 5242880 | tf_op jit(solution)/shard_map/all_to_all | solution.py:79
Sparse Core Ops, SparseCore 0:
  105.8 58.5 all-gather.1
